TPU v7x, 512 devices: a whole 4x8x8 slice. The times are simulated.
512 devices in a mesh: batch: 16 (over z_lo, x, core), seq: 32 (over y, z_hi).
Axes of the slice: x: 4, y: 8, z: 8 (z_hi: 4, z_lo: 2; z = z_hi * 2 + z_lo), core: 2. Of those that a mesh axis runs over, the one named last changes fastest.
Arguments:
- layer_inputs: bfloat16 [409600, 800], P(('batch', 'seq')), may hold values from -24 to 24
- output_grads: bfloat16 [409600, 800], P(('batch', 'seq')), may hold values from -48 to 48
- input_inverse: float32 [800, 200], replicated, may hold values from -1 to 3
- output_inverse: float32 [800, 200], replicated, may hold values from -1 to 3
Outputs:
- input_factor: float32 [800, 200], P('seq')
- output_factor: float32 [800, 200], P('seq')
- preconditioned: bfloat16 [800, 800], replicated
All inputs are finite; a program needn't handle non-finite values.
Results may differ from a plain program's by a relative error of at most 0.0075.
Values may be sent and summed in bfloat16 or wider, within the bound.
A program may use at most 64 MiB of HBM per device.

v0:
```python
import jax
import jax.numpy as jnp
from jax import lax
from jax.sharding import Mesh
from jax.sharding import PartitionSpec as P

BLOCK = 200
SEQ = ("seq_0", "seq_1")
BATCH_SEQ = ("batch", "seq_0", "seq_1")


def scatter_axes(x, axes, dim):
    if not axes:
        return x
    nearer = lax.psum_scatter(x, axes[0], scatter_dimension=dim, tiled=True)
    return scatter_axes(nearer, axes[1:], dim)


def sent_to_all(x, axis):
    peers = lax.axis_size(axis)
    return lax.all_to_all(jnp.broadcast_to(x[None], (peers, *x.shape)), axis, 0, 0, tiled=True)


def taken_together(x, axis):
    return sent_to_all(x, axis).sum(axis=0)


def together(arrays, axis):
    ends = [0]
    for a in arrays:
        ends.append(ends[-1] + a.size)
    subtotal = taken_together(jnp.concatenate([a.ravel() for a in arrays]), axis)
    return tuple((subtotal[b:e].reshape(a.shape) for a, b, e in zip(arrays, ends, ends[1:])))


def block_terms(values):
    tok_rows, width = values.shape
    stacked = values.reshape(tok_rows, width // BLOCK, BLOCK)
    product = jnp.einsum("tnb,tnc->nbc", stacked, stacked, preferred_element_type=jnp.float32)
    return product.reshape(width, BLOCK)


def reduce_terms(input_term, output_term, grad_term):
    shares = (
        scatter_axes(input_term.astype(jnp.bfloat16), SEQ, 0).astype(jnp.float32),
        scatter_axes(output_term.astype(jnp.bfloat16), SEQ, 0).astype(jnp.float32),
        scatter_axes(grad_term.astype(jnp.bfloat16), SEQ, 0).astype(jnp.float32),
    )
    return together((shares[0], shares[1], shares[2]), "batch")


def shards(layer_inputs, output_grads, input_inverse, output_inverse):
    tok_rows, in_width = layer_inputs.shape
    out_width = output_grads.shape[1]
    in_blocks = in_width // BLOCK
    out_blocks = out_width // BLOCK
    total_rows = tok_rows * lax.axis_size("batch") * lax.axis_size(SEQ)
    inverse_count = 1.0 / total_rows
    input_term = block_terms(layer_inputs)
    output_term = block_terms(output_grads)
    input_stack = input_inverse.reshape(in_blocks, BLOCK, BLOCK)
    output_stack = output_inverse.reshape(out_blocks, BLOCK, BLOCK)
    grad_term = lax.dot_general(
        layer_inputs, output_grads, (((0,), (0,)), ((), ())), preferred_element_type=jnp.float32
    )
    input_sum, output_sum, grad_sum = reduce_terms(input_term, output_term, grad_term)
    grad_owned = grad_sum * inverse_count
    owned_rows = grad_owned.shape[0]
    right_done = jnp.einsum(
        "rmk,mkl->rml",
        grad_owned.reshape(owned_rows, out_blocks, BLOCK),
        output_stack,
        precision=lax.Precision.HIGHEST,
    ).reshape(owned_rows, out_width)
    gathered = lax.all_gather(right_done, SEQ, axis=0, tiled=True)
    applied = jnp.einsum(
        "nij,njo->nio",
        input_stack,
        gathered.reshape(in_blocks, BLOCK, out_width),
        precision=lax.Precision.HIGHEST,
    ).reshape(in_width, out_width)
    preconditioned = applied.astype(jnp.bfloat16)
    input_factor = input_sum * inverse_count
    output_factor = output_sum * inverse_count
    return (input_factor, output_factor, preconditioned)


def solution(mesh):
    finer = Mesh(mesh.devices.reshape(mesh.shape["batch"], 8, 4), ("batch", "seq_0", "seq_1"))
    in_specs = (P(BATCH_SEQ, None), P(BATCH_SEQ, None), P(), P())
    out_specs = (P(SEQ, None), P(SEQ, None), P())
    return jax.shard_map(
        shards, mesh=finer, in_specs=in_specs, out_specs=out_specs, check_vma=False
    )
```

profile of v0, /device:TPU:1, one launch (start us, length us, event | category | flops | bytes accessed | tf_op | source)
XLA Modules:
  0.0 250.1 jit_solution(5033083344006876032)
XLA Ops:
  7.2 2.8 %copy.31 = bf16[800,800]{0,1:T(8,128)(2,1)S(1)} copy(bf16[800,800]{1,0:T(8,128)(2,1)} %param.4) | data formatting | bytes 2560000 | tf_op args[0]
  9.9 2.8 %copy.32 = bf16[800,800]{0,1:T(8,128)(2,1)S(1)} copy(bf16[800,800]{1,0:T(8,128)(2,1)} %param.5) | data formatting | bytes 2560000 | tf_op args[1]
  12.7 4.8 %convolution_convert_fusion.1 = bf16[800,800]{1,0:T(8,128)(2,1)} fusion(bf16[800,800]{1,0:T(8,128)(2,1)} %param.4, bf16[800,800]{1,0:T(8,128)(2,1)} %param.5), kind=kOutput, calls=%fused_computation.1 | convolution fusion | flops 1024640000 | bytes 3840000 | tf_op jit(solution)/shard_map/dot_general | solution.py:63
  17.4 0.6 convolution_convert_fusion.3
  18.1 0.6 convolution_convert_fusion.2
  18.7 32.7 %fusion.7 = (bf16[104,200]{1,0:T(8,128)(2,1)S(1)}, bf16[104,200]{1,0:T(8,128)(2,1)S(1)}, bf16[112,800]{1,0:T(8,128)(2,1)S(1)}) fusion(bf16[800,200]{1,0:T(8,128)(2,1)S(1)} %bitcast.40, bf16[800,200]{1,0:T(8,128)(2,1)S(1)} %bitcast.41, bf16[800,800]{1,0:T(8,128)(2,1)} %convolution_convert_fusion.1), kind=kCustom, calls=%all-reduce-scatter.6 | all-reduce-scatter fusion | flops 1049602 | bytes 2184448
  51.4 1.6 collective-permute-start
  53.0 2.2 collective-permute-start.2
  55.3 4.7 %collective-permute-start.4 = (bf16[84,800]{1,0:T(8,128)(2,1)S(1)}, bf16[84,800]{1,0:T(8,128)(2,1)S(1)}, u32[]{:S(2)}, u32[]{:S(2)}) collective-permute-start(bf16[84,800]{1,0:T(8,128)(2,1)S(1)} %slice.35), channel_id=1, source_target_pairs={{0,4},{4,8},{8,12},{12,16},{16,20},{20,24},{24,28},{1,5},{5,9},{9,... | collective-permute-start | bytes 403208
  59.9 1.3 dynamic-slice.14
  62.5 0.0 collective-permute-done
  62.5 0.2 concatenate.8
  62.8 0.0 collective-permute-done.2
  62.8 0.2 concatenate.10
  63.0 0.0 collective-permute-done.4
  63.0 0.7 concatenate.12
  63.7 0.1 constant_dynamic-slice_fusion.1
  63.8 18.1 %fusion.8 = (bf16[32,200]{1,0:T(8,128)(2,1)S(1)}, bf16[32,200]{1,0:T(8,128)(2,1)S(1)}, bf16[32,800]{1,0:T(8,128)(2,1)S(1)}) fusion(bf16[100,200]{1,0:T(8,128)(2,1)S(1)} %constant_dynamic-slice_fusion.5, bf16[100,200]{1,0:T(8,128)(2,1)S(1)} %constant_dynamic-slice_fusion.3, bf16[100,800]{1,0:T(8,128)(2,1)S(1)} %constant_dynamic-slice_fusion.1), kind=kCustom, calls=%all-reduce-scatter.7 | all-reduce-scatter fusion | flops 153601 | bytes 318848
  81.8 2.1 collective-permute-start.1
  84.0 1.3 dynamic-slice.18
  85.9 5.9 %collective-permute-start.3 = (bf16[21,200]{1,0:T(8,128)(2,1)S(1)}, bf16[21,200]{1,0:T(8,128)(2,1)S(1)}, u32[]{:S(2)}, u32[]{:S(2)}) collective-permute-start(bf16[21,200]{1,0:T(8,128)(2,1)S(1)} %slice.34), channel_id=1, source_target_pairs={{0,1},{1,2},{2,3},{4,5},{5,6},{6,7},{8,9},{9,10},{10,11},{12,13},{... | collective-permute-start | bytes 25208
  91.9 2.2 collective-permute-start.5
  94.1 0.0 collective-permute-done.1
  94.1 0.2 concatenate.9
  94.3 0.0 collective-permute-done.3
  94.3 0.2 concatenate.11
  94.5 0.1 reshape.76
  94.7 0.1 reshape.78
  94.8 0.4 collective-permute-done.5
  95.2 0.3 concatenate.13
  95.5 0.1 reshape.79
  95.6 0.1 concatenate.6
  95.8 2.3 broadcast_in_dim.2
  98.0 0.0 copy-start
  98.0 11.1 %all-to-all-start = ((f32[16,1,30000]{2,1,0:T(1,128)}), f32[16,1,30000]{2,1,0:T(1,128)S(1)}, u32[]{:S(2)}, u32[]{:S(2)}) async-start(f32[16,1,30000]{2,1,0:T(1,128)} %broadcast_in_dim.2), calls=%async_computation | async-start | bytes 3850240 | tf_op jit(solution)/shard_map/all_to_all | solution.py:21
  109.1 0.2 all-gather.3.cloned.1.call-start
  109.4 0.0 copy-done
  109.4 0.3 copy.38
  109.7 25.0 %all-to-all-done = f32[16,1,30000]{2,1,0:T(1,128)S(1)} async-done(((f32[16,1,30000]{2,1,0:T(1,128)}), f32[16,1,30000]{2,1,0:T(1,128)S(1)}, u32[]{:S(2)}, u32[]{:S(2)}) %all-to-all-start) | async-done | bytes 1920032 | tf_op jit(solution)/shard_map/all_to_all | solution.py:21
  134.7 1.2 reduce_sum.9
  135.9 0.0 copy-start.1
  135.9 0.1 slice_multiply_fusion
  136.0 0.2 mul.28
  136.2 0.6 convolution_bitcast_fusion
  136.8 0.1 copy.36
  136.9 0.8 reshape.84
  137.6 0.0 all-gather.3.cloned.1.call-update
  137.7 0.0 copy-done.1
  137.7 1.2 copy.39
  138.8 0.1 slice_multiply_fusion.1
  138.9 0.7 mul.23
  139.6 0.7 mul.25
  140.3 95.4 %all-gather.3.cloned.1.call-done = f32[32,25,800]{2,1,0:T(8,128)} async-done(((f32[1,25,800]{2,1,0:T(8,128)}), f32[32,25,800]{2,1,0:T(8,128)}) %all-gather.3.cloned.1.call-update) | async-done | bytes 2560016 | tf_op jit(solution)/shard_map/all_gather | solution.py:75
  235.8 2.2 reshape.82
  238.0 5.3 %convolution_convert_fusion = bf16[4,800,200]{1,2,0:T(8,128)(2,1)} fusion(f32[4,200,800]{2,1,0:T(8,128)S(1)} %reshape.82, f32[4,200,200]{2,1,0:T(8,128)} %bitcast.38), kind=kOutput, calls=%fused_computation | convolution fusion | flops 1536640000 | bytes 4480000 | tf_op jit(solution)/shard_map/nij,njo->nio/dot_general | solution.py:76
  (11 shorter events, 0.2 us)
Async XLA Ops:
  51.4 11.1 %collective-permute-start = (bf16[28,200]{1,0:T(8,128)(2,1)S(1)}, bf16[28,200]{1,0:T(8,128)(2,1)S(1)}, u32[]{:S(2)}, u32[]{:S(2)}) collective-permute-start(bf16[28,200]{1,0:T(8,128)(2,1)S(1)} %slice.31), channel_id=1, source_target_pairs={{0,4},{4,8},{8,12},{12,16},{16,20},{20,24},{24,28},{1,5},{5,9},{9,... | collective-permute-start | bytes 33608
  53.0 9.8 %collective-permute-start.2 = (bf16[28,200]{1,0:T(8,128)(2,1)S(1)}, bf16[28,200]{1,0:T(8,128)(2,1)S(1)}, u32[]{:S(2)}, u32[]{:S(2)}) collective-permute-start(bf16[28,200]{1,0:T(8,128)(2,1)S(1)} %slice.33), channel_id=1, source_target_pairs={{0,4},{4,8},{8,12},{12,16},{16,20},{20,24},{24,28},{1,5},{5,9},{9,... | collective-permute-start | bytes 33608
  55.3 7.8 %collective-permute-start.4 = (bf16[84,800]{1,0:T(8,128)(2,1)S(1)}, bf16[84,800]{1,0:T(8,128)(2,1)S(1)}, u32[]{:S(2)}, u32[]{:S(2)}) collective-permute-start(bf16[84,800]{1,0:T(8,128)(2,1)S(1)} %slice.35), channel_id=1, source_target_pairs={{0,4},{4,8},{8,12},{12,16},{16,20},{20,24},{24,28},{1,5},{5,9},{9,... | collective-permute-start | bytes 403208
  81.8 12.2 %collective-permute-start.1 = (bf16[21,200]{1,0:T(8,128)(2,1)S(1)}, bf16[21,200]{1,0:T(8,128)(2,1)S(1)}, u32[]{:S(2)}, u32[]{:S(2)}) collective-permute-start(bf16[21,200]{1,0:T(8,128)(2,1)S(1)} %slice.32), channel_id=1, source_target_pairs={{0,1},{1,2},{2,3},{4,5},{5,6},{6,7},{8,9},{9,10},{10,11},{12,13},{... | collective-permute-start | bytes 25208
  85.9 8.4 %collective-permute-start.3 = (bf16[21,200]{1,0:T(8,128)(2,1)S(1)}, bf16[21,200]{1,0:T(8,128)(2,1)S(1)}, u32[]{:S(2)}, u32[]{:S(2)}) collective-permute-start(bf16[21,200]{1,0:T(8,128)(2,1)S(1)} %slice.34), channel_id=1, source_target_pairs={{0,1},{1,2},{2,3},{4,5},{5,6},{6,7},{8,9},{9,10},{10,11},{12,13},{... | collective-permute-start | bytes 25208
  91.9 3.3 %collective-permute-start.5 = (bf16[21,800]{1,0:T(8,128)(2,1)S(1)}, bf16[21,800]{1,0:T(8,128)(2,1)S(1)}, u32[]{:S(2)}, u32[]{:S(2)}) collective-permute-start(bf16[21,800]{1,0:T(8,128)(2,1)S(1)} %slice.36), channel_id=1, source_target_pairs={{0,1},{1,2},{2,3},{4,5},{5,6},{6,7},{8,9},{9,10},{10,11},{12,13},{... | collective-permute-start | bytes 100808
  98.0 11.3 %copy-start = (f32[800,200]{0,1:T(8,128)S(1)}, f32[800,200]{0,1:T(8,128)}, u32[]{:S(2)}) copy-start(f32[800,200]{0,1:T(8,128)} %param.7) | copy-start | bytes 1920004
  98.0 36.6 %all-to-all-start = ((f32[16,1,30000]{2,1,0:T(1,128)}), f32[16,1,30000]{2,1,0:T(1,128)S(1)}, u32[]{:S(2)}, u32[]{:S(2)}) async-start(f32[16,1,30000]{2,1,0:T(1,128)} %broadcast_in_dim.2), calls=%async_computation | async-start | bytes 3850240 | tf_op jit(solution)/shard_map/all_to_all | solution.py:21
  109.1 126.6 %all-gather.3.cloned.1.call-start = ((), (), s32[]{:S(2)}) async-start(), calls=%async_computation.1 | async-start | bytes 3784704 | tf_op jit(solution)/shard_map/all_gather | solution.py:75
  135.9 1.8 copy-start.1
Sparse Core Ops, SparseCore 0:
  137.8 97.9 all-gather.2
where the time goes:
time: 251 us; the launch traced here: 250 us
  waiting for transfers between devices  121 us (48%)
  blocking collectives  50.7 us (20%)
  starting transfers between devices  30 us (12%)
  local copies, waits for them, and re-layouts  18.9 us (8%)
  between operations  16.4 us (7%)
  matrix products  11.8 us (5%)
    all_gather x1, waiting for transfers between devices, shards(): gathered = lax.all_gather(right_done, SEQ, axis=0, tiled=True)  95.4 us
    unnamed x2, blocking collectives  50.7 us
    all_to_all x1, waiting for transfers between devices, sent_to_all(): lax.all_to_all(jnp.broadcast_to(x[None], (peers, *x.shape)), axis, 0, 0,...  25 us
    unnamed x6, starting transfers between devices  18.7 us
    all_to_all x1, starting transfers between devices, sent_to_all(): lax.all_to_all(jnp.broadcast_to(x[None], (peers, *x.shape)), axis, 0, 0,...  11.1 us
    unnamed x27, local copies, waits for them, and re-layouts  10.8 us
    dot_general x1, matrix products, shards(): jnp.einsum('nij,njo->nio', input_stack, gathered.reshape(in_blocks, BLOCK...  5.26 us
  transfers between devices with their start and end apart: 8, of which 3 were waited for; matrix products, arithmetic and copies ran while one was open for 3% of the time, Pallas kernels for 0%

commit v1 on v0

v1 whole, which is shorter than its diff:
```python
import functools

import jax
import jax.numpy as jnp
from jax import lax
from jax.experimental import pallas as pl
from jax.experimental.pallas import tpu as pltpu
from jax.sharding import PartitionSpec as P

BLOCK = 200
MESH = pl.DeviceIdType.MESH
NX, NA, NB = 4, 8, 8
PLANE = NX * NA
ROWS = 40
LANES = 128
F32 = jnp.float32
BF16 = jnp.bfloat16
PIECES = ((0, 56), (56, 48), (104, 48), (152, 48))


def nn(l, r):
    return lax.dot_general(l, r, (((1,), (0,)), ((), ())), preferred_element_type=F32)


def nt(l, r):
    return lax.dot_general(l, r, (((1,), (1,)), ((), ())), preferred_element_type=F32)


def tn(l, r):
    return lax.dot_general(l, r, (((0,), (0,)), ((), ())), preferred_element_type=F32)


def split(m):
    hi = m.astype(BF16)
    return hi, (m - hi.astype(F32)).astype(BF16)


def kernel(inverse_count, x_h, g_h, p_h, q_h, inf_ref, outf_ref, pre_ref,
           xg, pv, qv, xt, gq, gs, gr, rs, rr, ar, ag, cs, cr, cacc, crs, crr, car, fown, cfin,
           ld, gs_s, gs_r, rs_s, rs_r, ar_s, ar_r, ag_s, ag_r, fw_s, fw_r,
           cd_s, cd_r, cs_s, cs_r, ca_s, ca_r, cf_s, cf_r):
    bt = lax.axis_index("batch")
    sq = lax.axis_index("seq")
    core = lax.rem(bt, 2)
    x = lax.rem(lax.div(bt, 2), 4)
    zl = lax.div(bt, 8)
    y = lax.div(sq, 4)
    zh = lax.rem(sq, 4)
    z = 2 * zh + zl
    a = y + core * (z - y)
    b = z + core * (y - z)
    me = 4 * a + x
    other = 1 - core

    def device(x2, a2, b2):
        y2 = a2 + core * (b2 - a2)
        z2 = b2 + core * (a2 - b2)
        return lax.rem(z2, 2) * 8 + x2 * 2 + core, y2 * 4 + lax.div(z2, 2)

    def plane(d):
        x2 = lax.rem(x + lax.rem(d, 4), 4)
        a2 = lax.rem(a + lax.div(d, 4), 8)
        return 4 * a2 + x2, device(x2, a2, b)

    def plane_from(d):
        x2 = lax.rem(x - lax.rem(d, 4) + 4, 4)
        a2 = lax.rem(a - lax.div(d, 4) + 8, 8)
        return 4 * a2 + x2

    def line(d):
        return device(x, a, lax.rem(b + d, 8))

    def each(lo, hi, f):
        def step(i, c):
            f(i)
            return c
        lax.fori_loop(lo, hi, step, 0)

    partner = (bt + 1 - 2 * core, sq)

    def remote(src, dst, s, r, dev):
        return pltpu.make_async_remote_copy(src_ref=src, dst_ref=dst, send_sem=s, recv_sem=r,
                                            device_id=dev, device_id_type=MESH)

    def drain(ref, sem):
        pltpu.make_async_copy(ref, ref, sem).wait()

    loads = [
        pltpu.make_async_copy(x_h, xg.at[0], ld.at[0]),
        pltpu.make_async_copy(p_h, pv, ld.at[1]),
        pltpu.make_async_copy(g_h, xg.at[1], ld.at[2]),
        pltpu.make_async_copy(q_h, qv, ld.at[3]),
    ]
    for c in loads:
        c.start()

    barrier = pltpu.get_barrier_semaphore()

    def hello(dev):
        pl.semaphore_signal(barrier, inc=1, device_id=dev, device_id_type=MESH)

    each(1, PLANE, lambda d: hello(plane(d)[1]))
    each(1, NB, lambda d: hello(line(d)))
    each(1, 16, lambda d: hello((lax.rem(bt + d, 16), sq)))

    cacc[...] = jnp.zeros_like(cacc)
    gq[:, 768:896] = jnp.zeros((800, 128), BF16)

    loads[0].wait()
    loads[1].wait()
    for i in range(4):
        hi, lo = split(pv[200 * i:200 * i + 200, :])
        xi = xg[0, :, 200 * i:200 * i + 200]
        xt[i] = (nt(hi, xi) + nt(lo, xi)).astype(BF16)
    loads[2].wait()
    loads[3].wait()
    for j in range(4):
        hi, lo = split(qv[200 * j:200 * j + 200, :])
        gj = xg[1, :, 200 * j:200 * j + 200]
        gq[:, 200 * j:200 * j + 200] = (nn(gj, hi) + nn(gj, lo)).astype(BF16)

    def strips(i):
        lhs = xt[i]
        for n in range(3):
            acc = nn(lhs, gq[:, 256 * n:256 * n + 256])
            for half in range(2):
                yield (10 * n + 5 * half, 5), acc[:, 128 * half:128 * half + 128].reshape(5, ROWS, LANES)
        acc = nn(lhs, gq[:, 768:896])
        packed = jnp.zeros((80, LANES), F32)
        for n, (r0, rn) in enumerate(PIECES):
            piece = jnp.concatenate([acc[r0:r0 + rn], jnp.zeros((80 - rn, LANES), F32)], axis=0)
            packed += pltpu.roll(piece, 32 * n, 1) if n else piece
        yield (30, 2), packed.reshape(2, ROWS, LANES)

    for ii in range(2):
        for (k, n), part in strips(2 * other + ii):
            gs[ii, k:k + n] = part.astype(BF16)
        if ii == 0:
            pl.semaphore_wait(barrier, (PLANE - 1) + (NB - 1) + 15)
        remote(gs.at[ii], gr.at[ii], gs_s.at[ii], gs_r.at[ii], partner).start()

    for ii in range(2):
        first = True
        for (k, n), part in strips(2 * core + ii):
            if first:
                drain(gr.at[ii], gs_r.at[ii])
                first = False
            rs[ii, k:k + n] = (part + gr[ii, k:k + n].astype(F32)).astype(BF16)

        def send(d, ii=ii):
            k, dev = plane(d)
            remote(rs.at[ii, k], rr.at[ii, d - 1], rs_s.at[ii], rs_r.at[ii], dev).start()
        each(1, PLANE, send)

    for n in range(4):
        t = xg[other, :, 200 * n:200 * n + 200]
        cs[n, :, 0:200] = tn(t, t).astype(BF16)
    remote(cs, cr, cd_s, cd_r, partner).start()
    for n in range(4):
        t = xg[core, :, 200 * n:200 * n + 200]
        c = tn(t, t)
        if n == 0:
            drain(cr, cd_r)
        cacc[0:200, 0:200] = c + cr[n, :, 0:200].astype(F32)
        for m in range(8):
            s = 8 * n + m
            s1 = 8 * (s % 4) + 4 * (s // 16) + (s // 4) % 4
            k = s + core * (s1 - s)
            crs[k] = cacc[25 * m:25 * m + 32, :].astype(BF16)

    def send_factor(d):
        k, dev = plane(d)
        remote(crs.at[k], crr.at[d - 1], cs_s, cs_r, dev).start()
    each(1, PLANE, send_factor)

    def summed(own, rest, count):
        acc = own.astype(F32)
        for d in range(count):
            acc = acc + rest(d).astype(F32)
        return acc

    for ii in range(2):
        drain(rr.at[ii], rs_r.at[ii])
        ar[ii, b] = summed(rs[ii, me], lambda d: rr[ii, d], PLANE - 1).astype(BF16)

        def send_line(d, ii=ii):
            remote(ar.at[ii, b], ar.at[ii, b], ar_s.at[ii], ar_r.at[ii, b], line(d)).start()
        each(1, NB, send_line)

    drain(crr, cs_r)
    car[b] = summed(crs[me], lambda d: crr[d], PLANE - 1).astype(BF16)

    def send_factor_line(d):
        remote(car.at[b], car.at[b], ca_s, ca_r.at[b], line(d)).start()
    each(1, NB, send_factor_line)

    for ii in range(2):
        def got(d, ii=ii):
            b2 = lax.rem(b + d, 8)
            drain(ar.at[ii, b2], ar_r.at[ii, b2])
        each(1, NB, got)
        total = summed(ar[ii, 0], lambda d: ar[ii, d + 1], NB - 1)
        ag[core, ii, me] = (total * inverse_count).astype(BF16)

        def send_out(d, ii=ii):
            k, dev = plane(d)
            mine = ag.at[core, ii, me]
            remote(mine, mine, ag_s.at[ii], ag_r.at[ii, me], dev).start()
        each(1, PLANE, send_out)
        mine = ag.at[core, ii, me]
        remote(mine, mine, fw_s.at[ii], fw_r.at[ii], partner).start()

    def got_factor(d):
        b2 = lax.rem(b + d, 8)
        drain(car.at[b2], ca_r.at[b2])
    each(1, NB, got_factor)
    fown[...] = summed(car[0], lambda d: car[d + 1], NB - 1) * inverse_count

    in_holder = jnp.logical_and(core == 0, x == zh)
    out_holder = jnp.logical_and(core == 1, y == 4 * zl + x)

    def send_in(d):
        dev = (8 * zl + lax.rem(lax.rem(bt, 8) + d, 8), sq)
        remote(fown, cfin.at[0], cf_s, cf_r.at[0], dev).start()

    def send_outf(d):
        remote(fown, cfin.at[1], cf_s, cf_r.at[1], (lax.rem(bt + d, 16), sq)).start()

    @pl.when(in_holder)
    def _():
        each(1, 8, send_in)
        cfin[0] = fown[...]

    @pl.when(out_holder)
    def _():
        each(1, 16, send_outf)
        cfin[1] = fown[...]

    for ii in range(2):
        def forward(d, ii=ii):
            k = plane_from(d)
            block = ag.at[core, ii, k]
            drain(block, ag_r.at[ii, k])
            remote(block, block, fw_s.at[ii], fw_r.at[ii], partner).start()
        each(1, PLANE, forward)

    def assemble(c, ii):
        row = 200 * (2 * c + ii)
        for j in range(6):
            pre_ref[pl.ds(row, 200), 128 * j:128 * j + 128] = ag[c, ii, 5 * j:5 * j + 5].reshape(200, LANES)
        tail = ag[c, ii, 30:32].reshape(80, LANES).astype(F32)
        for n, (r0, rn) in enumerate(PIECES):
            piece = pltpu.roll(tail, 128 - 32 * n, 1) if n else tail
            pre_ref[pl.ds(row + r0, rn), 768:800] = piece[0:rn, 0:32].astype(BF16)

    for ii in range(2):
        drain(ag.at[other, ii], fw_r.at[ii])
    for c in range(2):
        for ii in range(2):
            assemble(c, ii)

    @pl.when(jnp.logical_not(in_holder))
    def _():
        drain(cfin.at[0], cf_r.at[0])

    @pl.when(jnp.logical_not(out_holder))
    def _():
        drain(cfin.at[1], cf_r.at[1])

    inf_ref[...] = cfin[0, 0:25, 0:200]
    outf_ref[...] = cfin[1, 0:25, 0:200]

    for ii in range(2):
        drain(gs.at[ii], gs_s.at[ii])
        drain(rr.at[ii], rs_s.at[ii])
        drain(ar.at[ii, 0:NB - 1], ar_s.at[ii])
        drain(ag.at[core, ii, 0:PLANE - 1], ag_s.at[ii])
        drain(ag.at[core, ii], fw_s.at[ii])
    drain(cs, cd_s)
    drain(crr, cs_s)
    drain(car.at[0:NB - 1], ca_s)

    @pl.when(in_holder)
    def _():
        each(0, 7, lambda d: drain(fown, cf_s))

    @pl.when(out_holder)
    def _():
        each(0, 15, lambda d: drain(fown, cf_s))


def shards(total_rows, layer_inputs, output_grads, input_inverse, output_inverse):
    dma = pltpu.SemaphoreType.DMA
    any_space = pl.BlockSpec(memory_space=pltpu.HBM)
    vmem = pl.BlockSpec(memory_space=pltpu.VMEM)
    return pl.pallas_call(
        functools.partial(kernel, 1.0 / total_rows),
        out_shape=(
            jax.ShapeDtypeStruct((25, 200), F32),
            jax.ShapeDtypeStruct((25, 200), F32),
            jax.ShapeDtypeStruct((800, 800), BF16),
        ),
        in_specs=[any_space] * 4,
        out_specs=(vmem, vmem, vmem),
        scratch_shapes=[
            pltpu.VMEM((2, 800, 800), BF16),
            pltpu.VMEM((800, 200), F32),
            pltpu.VMEM((800, 200), F32),
            pltpu.VMEM((4, 200, 800), BF16),
            pltpu.VMEM((800, 896), BF16),
            pltpu.VMEM((2, PLANE, ROWS, LANES), BF16),
            pltpu.VMEM((2, PLANE, ROWS, LANES), BF16),
            pltpu.VMEM((2, PLANE, ROWS, LANES), BF16),
            pltpu.VMEM((2, PLANE - 1, ROWS, LANES), BF16),
            pltpu.VMEM((2, NB, ROWS, LANES), BF16),
            pltpu.VMEM((2, 2, PLANE, ROWS, LANES), BF16),
            pltpu.VMEM((4, 200, 256), BF16),
            pltpu.VMEM((4, 200, 256), BF16),
            pltpu.VMEM((208, 256), F32),
            pltpu.VMEM((PLANE, 32, 256), BF16),
            pltpu.VMEM((PLANE - 1, 32, 256), BF16),
            pltpu.VMEM((NB, 32, 256), BF16),
            pltpu.VMEM((32, 256), F32),
            pltpu.VMEM((2, 32, 256), F32),
            dma((4,)),
            dma((2,)), dma((2,)), dma((2,)), dma((2,)),
            dma((2,)), dma((2, NB)), dma((2,)), dma((2, PLANE)), dma((2,)), dma((2,)),
            dma, dma, dma, dma, dma, dma((NB,)), dma, dma((2,)),
        ],
        compiler_params=pltpu.CompilerParams(
            collective_id=0, has_side_effects=True, vmem_limit_bytes=48 * 1024 * 1024
        ),
    )(layer_inputs, output_grads, input_inverse, output_inverse)


def solution(mesh):
    both = P(("batch", "seq"), None)
    return jax.shard_map(
        functools.partial(shards, 800 * mesh.size), mesh=mesh,
        in_specs=(both, both, P(), P()),
        out_specs=(P("seq", None), P("seq", None), P()),
        check_vma=False,
    )
```

time: 251 us -> 59.8 us (0.24)
  waiting for transfers between devices: 121 us -> 0 us
  Pallas kernels: 0 us -> 52.4 us
  blocking collectives: 50.7 us -> 0 us
  starting transfers between devices: 30 us -> 0 us
  between operations: 16.4 us -> 0.68 us
  local copies, waits for them, and re-layouts: 18.9 us -> 6.56 us
  matrix products: 11.8 us -> 0 us
    all_gather x1 -> x0, waiting for transfers between devices: 95.4 us -> none  [shards(): gathered = lax.all_gather(right_done, SEQ, axis=0, tiled=True)]
    pallas_call x0 -> x1, Pallas kernels: none -> 52.4 us  [shards(): pl.pallas_call(functools.partial(kernel, 1.0 / total_rows), out_shape=(ja...]
    unnamed x2 -> x0, blocking collectives: 50.7 us -> none
    all_to_all x1 -> x0, waiting for transfers between devices: 25 us -> none  [sent_to_all(): lax.all_to_all(jnp.broadcast_to(x[None], (peers, *x.shape)), axis, 0, 0,...]
    unnamed x6 -> x0, starting transfers between devices: 18.7 us -> none
    dot_general x5 -> x0, matrix products: 11.8 us -> none  [the longest x1 5.26 us: shards(): jnp.einsum('nij,njo->nio', input_stack, gathered.reshape(in_blocks, BLOCK...]
    all_to_all x1 -> x0, starting transfers between devices: 11.1 us -> none  [sent_to_all(): lax.all_to_all(jnp.broadcast_to(x[None], (peers, *x.shape)), axis, 0, 0,...]
    unnamed x27 -> x9, local copies, waits for them, and re-layouts: 10.8 us -> 6.56 us
  transfers between devices with their start and end apart: 8 -> 0, of which waited for: 3 -> 0; matrix products, arithmetic and copies ran while one was open for 3% -> 0% of each run, Pallas kernels for 0% -> 0%
where the time goes in v1:
time: 59.8 us; the launch traced here: 59.6 us
  Pallas kernels  52.4 us (88%)
  local copies, waits for them, and re-layouts  6.56 us (11%)
  between operations  0.68 us (1%)
    pallas_call x1, Pallas kernels, shards(): pl.pallas_call(functools.partial(kernel, 1.0 / total_rows), out_shape=(ja...  52.4 us
    unnamed x9, local copies, waits for them, and re-layouts  6.56 us

profile of v1, /device:TPU:1, one launch (start us, length us, event | category | flops | bytes accessed | tf_op | source)
XLA Modules:
  0.0 59.6 jit_solution(13379986288122163675)
XLA Ops:
  0.6 0.0 copy-start
  0.6 1.5 %copy.7.p_h = f32[800,200]{1,0:T(8,128)S(1)} copy(f32[800,200]{0,1:T(8,128)} %param.6) | data formatting | bytes 1280000 | tf_op args[2]
  2.1 1.4 %copy.8.q_h = f32[800,200]{1,0:T(8,128)S(1)} copy(f32[800,200]{0,1:T(8,128)} %param.7) | data formatting | bytes 1280000 | tf_op args[3]
  3.5 0.0 copy-done
  3.5 0.0 copy-start.1
  3.5 1.4 %copy-done.1 = bf16[800,800]{1,0:T(8,128)(2,1)S(1)} copy-done((bf16[800,800]{1,0:T(8,128)(2,1)S(1)}, bf16[800,800]{1,0:T(8,128)(2,1)}, u32[]{:S(2)}) %copy-start.1) | copy-done | bytes 1280024
  4.9 52.4 %shard_map.67 = (f32[25,200]{1,0:T(8,128)S(1)}, f32[25,200]{1,0:T(8,128)S(1)}, bf16[800,800]{1,0:T(8,128)(2,1)S(1)}) custom-call(bf16[800,800]{1,0:T(8,128)(2,1)S(1)} %copy-done, bf16[800,800]{1,0:T(8,128)(2,1)S(1)} %copy-done.1, f32[800,200]{1,0:T(8,128)S(1)} %copy.7.p_h, f32[800,200]{1,0:T(8,128)S(1)} %copy.8.q_h), custom_call_target="tpu_custom_call" | custom-call | tf_op jit(solution)/shard_map/pallas_call | solution.py:296
  57.3 0.6 %copy.12 = f32[25,200]{1,0:T(8,128)} copy(f32[25,200]{1,0:T(8,128)S(1)} %get-tuple-element.6) | data formatting | bytes 40000
  57.9 0.6 %copy.13 = f32[25,200]{1,0:T(8,128)} copy(f32[25,200]{1,0:T(8,128)S(1)} %get-tuple-element.7) | data formatting | bytes 40000
  58.5 1.1 %copy.14 = bf16[800,800]{1,0:T(8,128)(2,1)} copy(bf16[800,800]{1,0:T(8,128)(2,1)S(1)} %get-tuple-element.8) | data formatting | bytes 2560000
Async XLA Ops:
  0.6 2.9 %copy-start = (bf16[800,800]{1,0:T(8,128)(2,1)S(1)}, bf16[800,800]{1,0:T(8,128)(2,1)}, u32[]{:S(2)}) copy-start(bf16[800,800]{1,0:T(8,128)(2,1)} %x_h.1) | copy-start | bytes 3840004
  3.5 1.4 %copy-start.1 = (bf16[800,800]{1,0:T(8,128)(2,1)S(1)}, bf16[800,800]{1,0:T(8,128)(2,1)}, u32[]{:S(2)}) copy-start(bf16[800,800]{1,0:T(8,128)(2,1)} %g_h.1) | copy-start | bytes 3840004

commit v2 on v1

v2 whole, which is shorter than its diff:
```python
import functools

import jax
import jax.numpy as jnp
from jax import lax
from jax.experimental import pallas as pl
from jax.experimental.pallas import tpu as pltpu
from jax.sharding import PartitionSpec as P

BLOCK = 200
MESH = pl.DeviceIdType.MESH
NX, NA, NB = 4, 8, 8
PLANE = NX * NA
ROWS = 40
LANES = 128
VMEM_LIMIT = 40 * 1024 * 1024
OFFSETS = sorted(((dx, da) for dx in range(NX) for da in range(NA) if dx or da),
                 key=lambda o: -(min(o[0], NX - o[0]) + min(o[1], NA - o[1])))
F32 = jnp.float32
BF16 = jnp.bfloat16
PIECES = ((0, 56), (56, 48), (104, 48), (152, 48))


def nn(l, r):
    return lax.dot_general(l, r, (((1,), (0,)), ((), ())), preferred_element_type=F32)


def nt(l, r):
    return lax.dot_general(l, r, (((1,), (1,)), ((), ())), preferred_element_type=F32)


def tn(l, r):
    return lax.dot_general(l, r, (((0,), (0,)), ((), ())), preferred_element_type=F32)


def split(m):
    hi = m.astype(BF16)
    return hi, (m - hi.astype(F32)).astype(BF16)


def kernel(inverse_count, x_h, g_h, p_h, q_h, inf_ref, outf_ref, pre_ref,
           xg, pv, qv, xt, gq, gs, gr, rs, rr, ar, ag, cs, cr, cacc, crs, crr, car, fown, cfin,
           ld, gs_s, gs_r, rs_s, rs_r, ar_s, ar_r, ag_s, ag_r, fw_s, fw_r,
           cd_s, cd_r, cs_s, cs_r, ca_s, ca_r, cf_s, cf_r):
    bt = lax.axis_index("batch")
    sq = lax.axis_index("seq")
    core = lax.rem(bt, 2)
    x = lax.rem(lax.div(bt, 2), 4)
    zl = lax.div(bt, 8)
    y = lax.div(sq, 4)
    zh = lax.rem(sq, 4)
    z = 2 * zh + zl
    a = y + core * (z - y)
    b = z + core * (y - z)
    me = 4 * a + x
    other = 1 - core

    def device(x2, a2, b2):
        y2 = a2 + core * (b2 - a2)
        z2 = b2 + core * (a2 - b2)
        return lax.rem(z2, 2) * 8 + x2 * 2 + core, y2 * 4 + lax.div(z2, 2)

    def plane(n):
        x2 = lax.rem(x + OFFSETS[n][0], NX)
        a2 = lax.rem(a + OFFSETS[n][1], NA)
        return 4 * a2 + x2, device(x2, a2, b)

    def plane_from(n):
        x2 = lax.rem(x - OFFSETS[n][0] + NX, NX)
        a2 = lax.rem(a - OFFSETS[n][1] + NA, NA)
        return 4 * a2 + x2

    def line(d):
        return device(x, a, lax.rem(b + d, 8))

    def each(lo, hi, f):
        def step(i, c):
            f(i)
            return c
        lax.fori_loop(lo, hi, step, 0)

    partner = (bt + 1 - 2 * core, sq)

    def remote(src, dst, s, r, dev):
        return pltpu.make_async_remote_copy(src_ref=src, dst_ref=dst, send_sem=s, recv_sem=r,
                                            device_id=dev, device_id_type=MESH)

    def drain(ref, sem):
        pltpu.make_async_copy(ref, ref, sem).wait()

    loads = [
        pltpu.make_async_copy(p_h, pv, ld.at[0]),
        pltpu.make_async_copy(x_h, xg.at[0], ld.at[1]),
        pltpu.make_async_copy(q_h, qv, ld.at[2]),
        pltpu.make_async_copy(g_h, xg.at[1], ld.at[3]),
    ]
    for c in loads:
        c.start()

    barrier = pltpu.get_barrier_semaphore()

    def hello(dev):
        pl.semaphore_signal(barrier, inc=1, device_id=dev, device_id_type=MESH)

    for n in range(PLANE - 1):
        hello(plane(n)[1])
    each(1, NB, lambda d: hello(line(d)))
    each(1, 16, lambda d: hello((lax.rem(bt + d, 16), sq)))

    cacc[...] = jnp.zeros_like(cacc)
    gq[:, 768:896] = jnp.zeros((800, 128), BF16)

    def xt_block(i):
        hi, lo = split(pv[:, 200 * i:200 * i + 200].T)
        xi = xg[0, :, 200 * i:200 * i + 200]
        xt[i] = (nt(hi, xi) + nt(lo, xi)).astype(BF16)

    def xt_half(ii, theirs):
        @pl.when(core == 0)
        def _():
            xt_block(ii + 2 * theirs)

        @pl.when(core == 1)
        def _():
            xt_block(ii + 2 - 2 * theirs)

    def strips(i):
        lhs = xt[i]
        for n in range(3):
            acc = nn(lhs, gq[:, 256 * n:256 * n + 256])
            for half in range(2):
                yield (10 * n + 5 * half, 5), acc[:, 128 * half:128 * half + 128].reshape(5, ROWS, LANES)
        acc = nn(lhs, gq[:, 768:896])
        packed = jnp.zeros((80, LANES), F32)
        for n, (r0, rn) in enumerate(PIECES):
            piece = jnp.concatenate([acc[r0:r0 + rn], jnp.zeros((80 - rn, LANES), F32)], axis=0)
            packed += pltpu.roll(piece, 32 * n, 1) if n else piece
        yield (30, 2), packed.reshape(2, ROWS, LANES)

    with jax.named_scope("xt0"):
        for c in loads[:2]:
            c.wait()
        xt_half(0, 1)
    with jax.named_scope("gq"):
        for c in loads[2:]:
            c.wait()
        for j in range(4):
            hi, lo = split(qv[:, 200 * j:200 * j + 200])
            gj = xg[1, :, 200 * j:200 * j + 200]
            gq[:, 200 * j:200 * j + 200] = (nt(gj, hi) + nt(gj, lo)).astype(BF16)

    for ii in range(2):
        with jax.named_scope("other%d" % ii):
            if ii == 1:
                xt_half(1, 1)
            for (k, n), part in strips(2 * other + ii):
                gs[ii, k:k + n] = part.astype(BF16)
        if ii == 0:
            with jax.named_scope("hello"):
                pl.semaphore_wait(barrier, (PLANE - 1) + (NB - 1) + 15)
        remote(gs.at[ii], gr.at[ii], gs_s.at[ii], gs_r.at[ii], partner).start()

    for ii in range(2):
        with jax.named_scope("xt_own%d" % ii):
            xt_half(ii, 0)
        with jax.named_scope("pair%d" % ii):
            drain(gr.at[ii], gs_r.at[ii])
        with jax.named_scope("own%d" % ii):
            for (k, n), part in strips(2 * core + ii):
                rs[ii, k:k + n] = (part + gr[ii, k:k + n].astype(F32)).astype(BF16)
        with jax.named_scope("send%d" % ii):
            for n in range(PLANE - 1):
                k, dev = plane(n)
                remote(rs.at[ii, k], rr.at[ii, n], rs_s.at[ii], rs_r.at[ii], dev).start()

    with jax.named_scope("cov_other"):
        for n in range(4):
            t = xg[other, :, 200 * n:200 * n + 200]
            cs[n, :, 0:200] = tn(t, t).astype(BF16)
        remote(cs, cr, cd_s, cd_r, partner).start()
    with jax.named_scope("cov_own"):
        for n in range(4):
            t = xg[core, :, 200 * n:200 * n + 200]
            c = tn(t, t)
            if n == 0:
                drain(cr, cd_r)
            cacc[0:200, 0:200] = c + cr[n, :, 0:200].astype(F32)
            for m in range(8):
                s = 8 * n + m
                s1 = 8 * (s % 4) + 4 * (s // 16) + (s // 4) % 4
                k = s + core * (s1 - s)
                crs[k] = cacc[25 * m:25 * m + 32, :].astype(BF16)
        for n in range(PLANE - 1):
            k, dev = plane(n)
            remote(crs.at[k], crr.at[n], cs_s, cs_r, dev).start()

    def summed(own, rest, count):
        acc = own.astype(F32)
        for d in range(count):
            acc = acc + rest(d).astype(F32)
        return acc

    for ii in range(2):
        with jax.named_scope("rs_wait%d" % ii):
            drain(rr.at[ii], rs_r.at[ii])
        with jax.named_scope("rs_sum%d" % ii):
            ar[ii, b] = summed(rs[ii, me], lambda d: rr[ii, d], PLANE - 1).astype(BF16)

            def send_line(d, ii=ii):
                remote(ar.at[ii, b], ar.at[ii, b], ar_s.at[ii], ar_r.at[ii, b], line(d)).start()
            each(1, NB, send_line)

    for ii in range(2):
        with jax.named_scope("ar_wait%d" % ii):
            def got(d, ii=ii):
                b2 = lax.rem(b + d, 8)
                drain(ar.at[ii, b2], ar_r.at[ii, b2])
            each(1, NB, got)
        with jax.named_scope("ar_sum%d" % ii):
            total = summed(ar[ii, 0], lambda d: ar[ii, d + 1], NB - 1)
            ag[core, ii, me] = (total * inverse_count).astype(BF16)
            mine = ag.at[core, ii, me]
            for n in range(PLANE - 1):
                remote(mine, mine, ag_s.at[ii], ag_r.at[ii, me], plane(n)[1]).start()
            remote(mine, mine, fw_s.at[ii], fw_r.at[ii], partner).start()

    with jax.named_scope("crs"):
        drain(crr, cs_r)
        car[b] = summed(crs[me], lambda d: crr[d], PLANE - 1).astype(BF16)

        def send_factor_line(d):
            remote(car.at[b], car.at[b], ca_s, ca_r.at[b], line(d)).start()
        each(1, NB, send_factor_line)

    def forward(ii):
        for n in range(PLANE - 1):
            k = plane_from(n)
            block = ag.at[core, ii, k]
            drain(block, ag_r.at[ii, k])
            remote(block, block, fw_s.at[ii], fw_r.at[ii], partner).start()

    with jax.named_scope("forward0"):
        forward(0)

    with jax.named_scope("car"):
        def got_factor(d):
            b2 = lax.rem(b + d, 8)
            drain(car.at[b2], ca_r.at[b2])
        each(1, NB, got_factor)
        fown[...] = summed(car[0], lambda d: car[d + 1], NB - 1) * inverse_count

    in_holder = jnp.logical_and(core == 0, x == zh)
    out_holder = jnp.logical_and(core == 1, y == 4 * zl + x)

    def send_in(d):
        dev = (8 * zl + lax.rem(lax.rem(bt, 8) + d, 8), sq)
        remote(fown, cfin.at[0], cf_s, cf_r.at[0], dev).start()

    def send_outf(d):
        remote(fown, cfin.at[1], cf_s, cf_r.at[1], (lax.rem(bt + d, 16), sq)).start()

    @pl.when(in_holder)
    def _():
        each(1, 8, send_in)
        cfin[0] = fown[...]

    @pl.when(out_holder)
    def _():
        each(1, 16, send_outf)
        cfin[1] = fown[...]

    with jax.named_scope("forward1"):
        forward(1)

    def assemble(c, ii):
        row = 200 * (2 * c + ii)
        for j in range(6):
            pre_ref[pl.ds(row, 200), 128 * j:128 * j + 128] = ag[c, ii, 5 * j:5 * j + 5].reshape(200, LANES)
        tail = ag[c, ii, 30:32].reshape(80, LANES).astype(F32)
        for n, (r0, rn) in enumerate(PIECES):
            piece = pltpu.roll(tail, 128 - 32 * n, 1) if n else tail
            pre_ref[pl.ds(row + r0, rn), 768:800] = piece[0:rn, 0:32].astype(BF16)

    for ii in range(2):
        with jax.named_scope("fw_wait%d" % ii):
            drain(ag.at[other, ii], fw_r.at[ii])
        with jax.named_scope("assemble%d" % ii):
            assemble(0, ii)
            assemble(1, ii)

    with jax.named_scope("factors"):
        @pl.when(jnp.logical_not(in_holder))
        def _():
            drain(cfin.at[0], cf_r.at[0])

        @pl.when(jnp.logical_not(out_holder))
        def _():
            drain(cfin.at[1], cf_r.at[1])

        inf_ref[...] = cfin[0, 0:25, 0:200]
        outf_ref[...] = cfin[1, 0:25, 0:200]

        for ii in range(2):
            drain(gs.at[ii], gs_s.at[ii])
            drain(rr.at[ii], rs_s.at[ii])
            drain(ar.at[ii, 0:NB - 1], ar_s.at[ii])
            drain(ag.at[core, ii, 0:PLANE - 1], ag_s.at[ii])
            drain(ag.at[core, ii], fw_s.at[ii])
        drain(cs, cd_s)
        drain(crr, cs_s)
        drain(car.at[0:NB - 1], ca_s)

    @pl.when(in_holder)
    def _():
        each(0, 7, lambda d: drain(fown, cf_s))

    @pl.when(out_holder)
    def _():
        each(0, 15, lambda d: drain(fown, cf_s))


def store(a_ref, b_ref, c_ref, a_h, b_h, c_h, sem):
    copies = [pltpu.make_async_copy(src, dst, sem.at[n])
              for n, (src, dst) in enumerate(((c_ref, c_h), (a_ref, a_h), (b_ref, b_h)))]
    for c in copies:
        c.start()
    for c in copies:
        c.wait()


def shards(total_rows, layer_inputs, output_grads, input_inverse, output_inverse):
    dma = pltpu.SemaphoreType.DMA
    hbm = pl.BlockSpec(memory_space=pltpu.HBM)
    vmem = pl.BlockSpec(memory_space=pltpu.VMEM)
    held = pl.pallas_call(
        functools.partial(kernel, 1.0 / total_rows),
        out_shape=(
            pltpu.VMEM((25, 200), F32),
            pltpu.VMEM((25, 200), F32),
            pltpu.VMEM((800, 800), BF16),
        ),
        in_specs=[hbm] * 4,
        out_specs=(vmem, vmem, vmem),
        scratch_shapes=[
            pltpu.VMEM((2, 800, 800), BF16),
            pltpu.VMEM((200, 800), F32),
            pltpu.VMEM((200, 800), F32),
            pltpu.VMEM((4, 200, 800), BF16),
            pltpu.VMEM((800, 896), BF16),
            pltpu.VMEM((2, PLANE, ROWS, LANES), BF16),
            pltpu.VMEM((2, PLANE, ROWS, LANES), BF16),
            pltpu.VMEM((2, PLANE, ROWS, LANES), BF16),
            pltpu.VMEM((2, PLANE - 1, ROWS, LANES), BF16),
            pltpu.VMEM((2, NB, ROWS, LANES), BF16),
            pltpu.VMEM((2, 2, PLANE, ROWS, LANES), BF16),
            pltpu.VMEM((4, 200, 256), BF16),
            pltpu.VMEM((4, 200, 256), BF16),
            pltpu.VMEM((208, 256), F32),
            pltpu.VMEM((PLANE, 32, 256), BF16),
            pltpu.VMEM((PLANE - 1, 32, 256), BF16),
            pltpu.VMEM((NB, 32, 256), BF16),
            pltpu.VMEM((32, 256), F32),
            pltpu.VMEM((2, 32, 256), F32),
            dma((4,)),
            dma((2,)), dma((2,)), dma((2,)), dma((2,)),
            dma((2,)), dma((2, NB)), dma((2,)), dma((2, PLANE)), dma((2,)), dma((2,)),
            dma, dma, dma, dma, dma, dma((NB,)), dma, dma((2,)),
        ],
        compiler_params=pltpu.CompilerParams(
            collective_id=0, has_side_effects=True, vmem_limit_bytes=VMEM_LIMIT
        ),
    )(*(pltpu.with_memory_space_constraint(v, pltpu.HBM) for v in (layer_inputs, output_grads, input_inverse.T, output_inverse.T)))
    return pl.pallas_call(
        store,
        out_shape=tuple(jax.ShapeDtypeStruct(h.shape, h.dtype) for h in held),
        in_specs=[vmem] * 3,
        out_specs=(hbm,) * 3,
        scratch_shapes=[dma((3,))],
        compiler_params=pltpu.CompilerParams(vmem_limit_bytes=4 * 1024 * 1024),
    )(*held)


def solution(mesh):
    both = P(("batch", "seq"), None)
    return jax.shard_map(
        functools.partial(shards, 800 * mesh.size), mesh=mesh,
        in_specs=(both, both, P(), P()),
        out_specs=(P("seq", None), P("seq", None), P()),
        check_vma=False,
    )
```

time: 59.8 us -> 50.5 us (0.84)
  local copies, waits for them, and re-layouts: 6.56 us -> 0 us
  Pallas kernels: 52.4 us -> 49.7 us
    unnamed x9 -> x0, local copies, waits for them, and re-layouts: 6.56 us -> none
    pallas_call x1 -> x2, Pallas kernels: 52.4 us -> 49.7 us  [the longest x1 48.6 us: shards(): pl.pallas_call(functools.partial(kernel, 1.0 / total_rows), out_shape=(pl...]
where the time goes in v2:
time: 50.5 us; the launch traced here: 50.3 us
  Pallas kernels  49.7 us (98%)
  between operations  0.64 us (1%)
    pallas_call x1, Pallas kernels, shards(): pl.pallas_call(functools.partial(kernel, 1.0 / total_rows), out_shape=(pl...  48.6 us
    pallas_call x1, Pallas kernels, shards(): pl.pallas_call(store, out_shape=tuple((jax.ShapeDtypeStruct(h.shape, h.dt...  1.13 us

profile of v2, /device:TPU:1, one launch (start us, length us, event | category | flops | bytes accessed | tf_op | source)
XLA Modules:
  0.0 50.3 jit_solution(15516245983857445759)
XLA Ops:
  0.6 48.6 %shard_map.67 = (f32[25,200]{1,0:T(8,128)S(1)}, f32[25,200]{1,0:T(8,128)S(1)}, bf16[800,800]{1,0:T(8,128)(2,1)S(1)}) custom-call(bf16[800,800]{1,0:T(8,128)(2,1)} %x_h.1, bf16[800,800]{1,0:T(8,128)(2,1)} %g_h.1, f32[200,800]{1,0:T(8,128)} %bitcast.2, f32[200,800]{1,0:T(8,128)} %bitcast.3), custom_call_target="tpu_custom_call" | custom-call | tf_op jit(solution)/shard_map/pallas_call | solution.py:335
  49.2 1.1 %shard_map.68 = (f32[25,200]{1,0:T(8,128)}, f32[25,200]{1,0:T(8,128)}, bf16[800,800]{1,0:T(8,128)(2,1)}) custom-call(f32[25,200]{1,0:T(8,128)S(1)} %get-tuple-element.6.a_ref, f32[25,200]{1,0:T(8,128)S(1)} %get-tuple-element.7.b_ref, bf16[800,800]{1,0:T(8,128)(2,1)S(1)} %get-tuple-element.8.c_ref), custom_call_target="tpu_custom_call" | custom-call | tf_op jit(solution)/shard_map/pallas_call | solution.py:373
